TPU v7x, 32 devices: a whole 2x2x4 slice. The times are simulated.
32 devices in a mesh: grp: 4 (over z), mem: 8 (over y, x, core).
Axes of the slice: x: 2, y: 2, z: 4, core: 2. Of those that a mesh axis runs over, the one named last changes fastest.
Arguments:
- embeddings: bfloat16 [32768, 4096], P(('grp', 'mem')), may hold values from -6 to 6
- local_picks: int32 [4, 64], P('grp', 'mem'), may hold values from 0 to 1023
- second_picks: int32 [4, 16], P('grp'), may hold values from 0 to 63
- final_picks: int32 [16], replicated, may hold values from 0 to 63
Outputs:
- gain_table: float32 [64, 64], P('grp', 'mem')
- final_cover: float32 [32768], P(('grp', 'mem'))
Inputs may be any that keep to these rules, and one draw needn't show every extreme that they name: `local_picks`: entry (g, m * 8 + k) names a row among the 1024 points of device m of group g; repeats may occur. `second_picks`: candidate indices of the group, in greedy order; repeats may occur. `final_picks`: index g * 16 + t names group g's second-round pick t; repeats may occur.
All inputs are finite; a program needn't handle non-finite values.
Results may differ from a plain program's by a relative error of at most 0.0003.
Values may be sent and summed in bfloat16 or wider, within the bound.
A program may use at most 64 MiB of HBM per device.

v0:
```python
import jax
import jax.numpy as jnp
from jax import lax
from jax.sharding import PartitionSpec as P

D = 4096


def per_device(embeddings, local_picks, second_picks, final_picks):
    scaling = float(D) ** (-0.5)
    point_count = embeddings.shape[0]
    local_count = local_picks.shape[1]
    second_list = second_picks[0]
    member = lax.axis_index("mem")
    choose = (local_picks[0][:, None] == lax.iota(jnp.int32, point_count)[None, :]).astype(
        jnp.bfloat16
    )
    own_rows = jnp.dot(choose, embeddings, preferred_element_type=jnp.float32).astype(jnp.bfloat16)

    def similar(other_rows):
        dims = (((1,), (1,)), ((), ()))
        return (
            lax.dot_general(embeddings, other_rows, dims, preferred_element_type=jnp.float32)
            * scaling
        )

    candidates = lax.all_gather(own_rows, "mem", axis=0, tiled=True)
    similar_map = similar(candidates)
    cand_total = candidates.shape[0]
    pick_table = (second_list[:, None] == lax.iota(jnp.int32, cand_total)[None, :]).astype(
        jnp.bfloat16
    )
    winners = jnp.dot(pick_table, candidates, preferred_element_type=jnp.float32).astype(
        jnp.bfloat16
    )
    union_rows = lax.all_gather(winners, "grp", axis=0, tiled=True)
    final_table = (
        final_picks[:, None] == lax.iota(jnp.int32, union_rows.shape[0])[None, :]
    ).astype(jnp.bfloat16)
    final_rows = jnp.dot(final_table, union_rows, preferred_element_type=jnp.float32).astype(
        jnp.bfloat16
    )
    own_block = lax.dynamic_slice_in_dim(similar_map, member * local_count, local_count, 1)
    coverage = jnp.max(own_block, axis=1)
    chosen_cols = jnp.take(similar_map, second_list, axis=1)

    def greedy_step(cover_now, column):
        partial_value = jnp.sum(jnp.maximum(similar_map - cover_now[:, None], 0.0), axis=0)
        return (jnp.maximum(cover_now, column), partial_value)

    _, partials = lax.scan(greedy_step, coverage, chosen_cols.T)
    gain_table = lax.psum_scatter(partials, "mem", scatter_dimension=1, tiled=True) / point_count
    final_cover = jnp.max(similar(final_rows), axis=1)
    return (gain_table, final_cover)


def solution(mesh):
    placed = (P(("grp", "mem"), None), P("grp", "mem"), P("grp", None), P())
    return jax.shard_map(
        per_device,
        mesh=mesh,
        in_specs=placed,
        out_specs=(P("grp", "mem"), P(("grp", "mem"))),
        check_vma=False,
    )
```

profile of v0, /device:TPU:0, one launch (start us, length us, event | category | flops | bytes accessed | tf_op | source)
XLA Modules:
  0.0 75.5 jit_solution(6943562138550951512)
XLA Ops:
  0.6 0.0 copy-start.2
  0.6 1.2 %dynamic-slice.4 = u32[1]{0:T(128)} dynamic-slice(u32[32]{0:T(128)} %constant.50, u32[]{:T(128)S(6)} %add.27), dynamic_slice_sizes={1} | dynamic-slice | bytes 12
  2.5 0.7 compare_and_fusion
  3.2 0.7 fusion.7
  3.9 0.0 copy-start
  3.9 4.8 %convolution_convert_fusion.2 = bf16[8,4096]{1,0:T(8,128)(2,1)S(1)} fusion(bf16[1024,4096]{1,0:T(8,128)(2,1)} %param.6, s32[8]{0:T(128)} %bitcast.25), kind=kOutput, calls=%fused_computation.5 | convolution fusion | flops 67149824 | bytes 8454176 | tf_op jit(solution)/shard_map/dot_general | solution.py:18
  8.7 11.3 %all_gather.6 = bf16[64,4096]{1,0:T(8,128)(2,1)S(1)} all-gather(bf16[8,4096]{1,0:T(8,128)(2,1)S(1)} %convolution_convert_fusion.2), channel_id=1, replica_groups=mesh['grp'=4,'mem'=8] {'mem'}, dimensions={0}, use_global_device_ids=true | all-gather | bytes 589824 | tf_op jit(solution)/shard_map/all_gather | solution.py:27
  20.0 0.0 copy-done.2
  20.0 0.2 convolution_convert_fusion.1
  20.2 0.0 copy-done
  20.3 0.0 copy-start.1
  20.3 2.7 %convolution_multiply_fusion = f32[64,1024]{1,0:T(8,128)S(1)} fusion(bf16[64,4096]{1,0:T(8,128)(2,1)S(1)} %all_gather.6, bf16[1024,4096]{1,0:T(8,128)(2,1)S(1)} %copy-done), kind=kOutput, calls=%fused_computation.6 | convolution fusion | flops 536936448 | bytes 9175040 | tf_op jit(solution)/shard_map/dot_general | solution.py:23
  23.0 0.6 gather_fusion
  23.5 0.1 broadcast_select_fusion
  23.6 0.2 copy.8
  23.8 4.8 %while.12 = (s32[]{:T(128)}, f32[1024]{0:T(1024)S(1)}, f32[16,64]{1,0:T(8,128)S(1)}, f32[16,1024]{1,0:T(8,128)S(1)}, f32[1024,64]{1,0:T(8,128)S(1)}, /*index=5*/s32[]{:T(128)}, s32[]{:T(128)}) while((s32[]{:T(128)}, f32[1024]{0:T(1024)S(1)}, f32[16,64]{1,0:T(8,128)S(1)}, f32[16,1024]{1,0:T(8,128)S(1)}, f32[1024,64]{1,0:T(8,128)S(1)}, ...), condition=%wide.region_3.4_spmd, body=%wide.region_1.0_spmd.sunk | while | flops 197570 | bytes 287581 | solution.py:51
  23.8 0.2 maximum_reduce_fusion.2
  24.1 0.2 maximum_reduce_fusion.2
  24.4 0.2 maximum_reduce_fusion.2
  24.7 0.2 maximum_reduce_fusion.2
  25.0 0.2 maximum_reduce_fusion.2
  25.3 0.2 maximum_reduce_fusion.2
  25.6 0.2 maximum_reduce_fusion.2
  25.9 0.2 maximum_reduce_fusion.2
  26.2 0.2 maximum_reduce_fusion.2
  26.5 0.2 maximum_reduce_fusion.2
  26.8 0.2 maximum_reduce_fusion.2
  27.1 0.2 maximum_reduce_fusion.2
  27.5 0.2 maximum_reduce_fusion.2
  27.8 0.2 maximum_reduce_fusion.2
  28.1 0.2 maximum_reduce_fusion.2
  28.4 0.2 maximum_reduce_fusion.2
  28.7 0.1 copy.9
  28.7 23.6 %all-reduce = f32[16,64]{0,1:T(8,128)S(1)} all-reduce(f32[16,64]{0,1:T(8,128)S(1)} %copy.9), channel_id=2, replica_groups=mesh['grp'=4,'mem'=8] {'mem'}, use_global_device_ids=true, to_apply=%region_4.5.clone | all-reduce | flops 1024 | bytes 8192
  52.3 0.6 dynamic-slice_multiply_fusion
  52.9 16.2 %all_gather.7 = bf16[64,4096]{1,0:T(8,128)(2,1)S(1)} all-gather(bf16[16,4096]{1,0:T(8,128)(2,1)S(1)} %convolution_convert_fusion.1), channel_id=1, replica_groups=mesh['grp'=4,'mem'=8] {'grp'}, dimensions={0}, use_global_device_ids=true | all-gather | bytes 655360 | tf_op jit(solution)/shard_map/all_gather | solution.py:36
  69.1 0.0 copy-done.1
  69.1 6.4 %fusion.2 = f32[1024]{0:T(1024)} fusion(bf16[1024,4096]{1,0:T(8,128)(2,1)} %param.6, bf16[64,4096]{1,0:T(8,128)(2,1)S(1)} %all_gather.7, s32[16]{0:T(128)S(1)} %copy-done.1), kind=kOutput, calls=%fused_computation.9 | convolution fusion | flops 142704640 | bytes 8917056 | tf_op jit(solution)/shard_map/dot_general | solution.py:23
  (51 shorter events, 0.9 us)
Async XLA Ops:
  0.6 19.4 %copy-start.2 = (s32[1,16]{1,0:T(1,128)S(1)}, s32[1,16]{1,0:T(1,128)}, u32[]{:S(2)}) copy-start(s32[1,16]{1,0:T(1,128)} %param.8) | copy-start | bytes 196
  3.9 16.4 %copy-start = (bf16[1024,4096]{1,0:T(8,128)(2,1)S(1)}, bf16[1024,4096]{1,0:T(8,128)(2,1)}, u32[]{:S(2)}) copy-start(bf16[1024,4096]{1,0:T(8,128)(2,1)} %param.6) | copy-start | bytes 25165828
  20.3 48.9 %copy-start.1 = (s32[16]{0:T(128)S(1)}, s32[16]{0:T(128)}, u32[]{:S(2)}) copy-start(s32[16]{0:T(128)} %param.9) | copy-start | bytes 196
where the time goes:
time: 75.8 us; the launch traced here: 75.5 us
  blocking collectives  51.1 us (67%)
  matrix products  14.1 us (19%)
  other arithmetic  5.58 us (7%)
  local copies, waits for them, and re-layouts  2.9 us (4%)
  between operations  1.36 us (2%)
    unnamed x1, blocking collectives  23.6 us
    all_gather x1, blocking collectives, per_device(): union_rows = lax.all_gather(winners, 'grp', axis=0, tiled=True)  16.2 us
    all_gather x1, blocking collectives, per_device(): candidates = lax.all_gather(own_rows, 'mem', axis=0, tiled=True)  11.3 us
    dot_general x2, matrix products, similar(): lax.dot_general(embeddings, other_rows, dims, preferred_element_type=jnp....  9.06 us
    dot_general x1, matrix products, per_device(): jnp.dot(choose, embeddings, preferred_element_type=jnp.float32)  4.78 us
    reduce_sum x16, other arithmetic, greedy_step(): jnp.sum(jnp.maximum(similar_map - cover_now[:, None], 0.0), axis=0)  3.49 us

commit v1 on v0

--- a/solution.py
+++ b/solution.py
@@ -4,6 +4,28 @@
 from jax.sharding import PartitionSpec as P
 
 D = 4096
+
+
+def in_order(pieces, dim):
+    shape = list(pieces.shape[1:])
+    shape[dim] *= pieces.shape[0]
+    return jnp.moveaxis(pieces, 0, dim).reshape(shape)
+
+
+def collect(value, axis, dim):
+    size = lax.axis_size(axis)
+    pairs = [(i, (i + 1) % size) for i in range(size)]
+    back = [(b, a) for a, b in pairs]
+    lower, upper = ([], [])
+    for hop in range(size - 1):
+        if hop % 2 == 0:
+            lower.append(lax.ppermute(lower[-1] if lower else value, axis, pairs))
+        else:
+            upper.append(lax.ppermute(upper[-1] if upper else value, axis, back))
+    blocks = jnp.stack([*lower[::-1], value, *upper])
+    shift = lax.axis_index(axis) - len(lower)
+    blocks = blocks[(jnp.arange(size) - shift) % size]
+    return in_order(blocks, dim)
 
 
 def per_device(embeddings, local_picks, second_picks, final_picks):
@@ -33,7 +55,7 @@
     winners = jnp.dot(pick_table, candidates, preferred_element_type=jnp.float32).astype(
         jnp.bfloat16
     )
-    union_rows = lax.all_gather(winners, "grp", axis=0, tiled=True)
+    union_rows = collect(winners, "grp", 0)
     final_table = (
         final_picks[:, None] == lax.iota(jnp.int32, union_rows.shape[0])[None, :]
     ).astype(jnp.bfloat16)

time: 75.8 us -> 62.3 us (0.82)
  blocking collectives: 51.1 us -> 34.9 us
  starting transfers between devices: 0 us -> 3.93 us
  other arithmetic: 5.58 us -> 4.36 us
    all_gather x1 -> x0, blocking collectives: 16.2 us -> none  [per_device(): union_rows = lax.all_gather(winners, 'grp', axis=0, tiled=True)]
    ppermute x0 -> x3, starting transfers between devices: none -> 3.93 us  [the longest x1 2.25 us: collect(): upper.append(lax.ppermute(upper[-1] if upper else value, axis, back))]
  transfers between devices with their start and end apart: 0 -> 3, of which waited for: 0 -> 0; matrix products, arithmetic and copies ran while one was open for 0% -> 15% of each run, Pallas kernels for 0% -> 0%
where the time goes in v1:
time: 62.3 us; the launch traced here: 62 us
  blocking collectives  34.9 us (56%)
  matrix products  14.1 us (23%)
  other arithmetic  4.36 us (7%)
  starting transfers between devices  3.93 us (6%)
  local copies, waits for them, and re-layouts  2.82 us (5%)
  between operations  1.45 us (2%)
    unnamed x1, blocking collectives  23.5 us
    all_gather x1, blocking collectives, per_device(): candidates = lax.all_gather(own_rows, 'mem', axis=0, tiled=True)  11.5 us
    dot_general x2, matrix products, similar(): lax.dot_general(embeddings, other_rows, dims, preferred_element_type=jnp....  9.06 us
    dot_general x1, matrix products, per_device(): jnp.dot(choose, embeddings, preferred_element_type=jnp.float32)  4.78 us
    reduce_sum x16, other arithmetic, greedy_step(): jnp.sum(jnp.maximum(similar_map - cover_now[:, None], 0.0), axis=0)  3.49 us
    ppermute x1, starting transfers between devices, collect(): upper.append(lax.ppermute(upper[-1] if upper else value, axis, back))  2.25 us
    ppermute x2, starting transfers between devices, collect(): lower.append(lax.ppermute(lower[-1] if lower else value, axis, pairs))  1.69 us
  transfers between devices with their start and end apart: 3, of which 0 were waited for; matrix products, arithmetic and copies ran while one was open for 15% of the time, Pallas kernels for 0%

profile of v1, /device:TPU:0, one launch (start us, length us, event | category | flops | bytes accessed | tf_op | source)
XLA Modules:
  0.0 62.0 jit_solution(16023083969853855764)
XLA Ops:
  0.6 0.0 slice-start
  0.6 0.0 copy-start.1
  0.7 0.0 slice-start.1
  0.7 4.8 %convolution_convert_fusion.2 = bf16[8,4096]{1,0:T(8,128)(2,1)S(1)} fusion(bf16[1024,4096]{1,0:T(8,128)(2,1)} %param.6, s32[8]{0:T(128)} %bitcast.39), kind=kOutput, calls=%fused_computation.6 | convolution fusion | flops 67149824 | bytes 8454176 | tf_op jit(solution)/shard_map/dot_general | solution.py:40
  5.4 11.5 %all_gather.3 = bf16[64,4096]{1,0:T(8,128)(2,1)S(1)} all-gather(bf16[8,4096]{1,0:T(8,128)(2,1)S(1)} %convolution_convert_fusion.2), channel_id=1, replica_groups=mesh['grp'=4,'mem'=8] {'mem'}, dimensions={0}, use_global_device_ids=true | all-gather | bytes 589824 | tf_op jit(solution)/shard_map/all_gather | solution.py:49
  16.9 0.0 copy-done.1
  16.9 0.2 convolution_convert_fusion.1
  17.1 1.6 %collective-permute-start = (bf16[16,4096]{1,0:T(8,128)(2,1)S(1)}, bf16[16,4096]{1,0:T(8,128)(2,1)S(1)}, u32[]{:S(2)}, u32[]{:S(2)}) collective-permute-start(bf16[16,4096]{1,0:T(8,128)(2,1)S(1)} %convolution_convert_fusion.1), channel_id=1, source_target_pairs={{0,8},{8,16},{16,24},{24,0},{1,9},{9,17},{17,25},{25,1},{2,10},{10... | collective-permute-start | bytes 393224 | tf_op jit(solution)/shard_map/ppermute | solution.py:22
  18.8 2.2 %collective-permute-start.2 = (bf16[16,4096]{1,0:T(8,128)(2,1)S(1)}, bf16[16,4096]{1,0:T(8,128)(2,1)S(1)}, u32[]{:S(2)}, u32[]{:S(2)}) collective-permute-start(bf16[16,4096]{1,0:T(8,128)(2,1)S(1)} %convolution_convert_fusion.1), channel_id=1, source_target_pairs={{8,0},{16,8},{24,16},{0,24},{9,1},{17,9},{25,17},{1,25},{10,2},{18... | collective-permute-start | bytes 393224 | tf_op jit(solution)/shard_map/ppermute | solution.py:24
  21.0 0.0 slice-done
  21.0 0.0 slice-done.1
  21.0 0.0 copy-start.2
  21.0 0.0 copy-start
  21.0 2.7 %convolution_multiply_fusion = f32[64,1024]{1,0:T(8,128)S(1)} fusion(bf16[64,4096]{1,0:T(8,128)(2,1)S(1)} %all_gather.3, bf16[1024,4096]{1,0:T(8,128)(2,1)S(1)} %bitcast.29), kind=kOutput, calls=%fused_computation.7 | convolution fusion | flops 536936448 | bytes 9175040 | tf_op jit(solution)/shard_map/dot_general | solution.py:45
  23.8 0.2 copy.8
  24.0 0.6 gather_fusion
  24.6 0.1 broadcast_select_fusion
  24.7 4.8 %while.12 = (s32[]{:T(128)}, f32[1024]{0:T(1024)S(1)}, f32[16,64]{1,0:T(8,128)S(1)}, f32[16,1024]{1,0:T(8,128)S(1)}, f32[1024,64]{1,0:T(8,128)S(1)}, /*index=5*/s32[]{:T(128)}, s32[]{:T(128)}) while((s32[]{:T(128)}, f32[1024]{0:T(1024)S(1)}, f32[16,64]{1,0:T(8,128)S(1)}, f32[16,1024]{1,0:T(8,128)S(1)}, f32[1024,64]{1,0:T(8,128)S(1)}, ...), condition=%wide.region_3.4_spmd, body=%wide.region_1.3_spmd.sunk | while | flops 197570 | bytes 287573 | solution.py:73
  24.7 0.2 maximum_reduce_fusion.2
  25.0 0.2 maximum_reduce_fusion.2
  25.3 0.2 maximum_reduce_fusion.2
  25.6 0.2 maximum_reduce_fusion.2
  25.9 0.2 maximum_reduce_fusion.2
  26.2 0.2 maximum_reduce_fusion.2
  26.5 0.2 maximum_reduce_fusion.2
  26.8 0.2 maximum_reduce_fusion.2
  27.1 0.2 maximum_reduce_fusion.2
  27.4 0.2 maximum_reduce_fusion.2
  27.7 0.2 maximum_reduce_fusion.2
  28.0 0.2 maximum_reduce_fusion.2
  28.3 0.2 maximum_reduce_fusion.2
  28.6 0.2 maximum_reduce_fusion.2
  28.9 0.2 maximum_reduce_fusion.2
  29.2 0.2 maximum_reduce_fusion.2
  29.5 0.0 collective-permute-done
  29.5 0.1 collective-permute-start.1
  29.6 0.1 copy.9
  29.7 0.0 copy-done.2
  29.7 0.6 dynamic-slice.4
  30.9 23.5 %all-reduce = f32[16,64]{0,1:T(8,128)S(1)} all-reduce(f32[16,64]{0,1:T(8,128)S(1)} %copy.9), channel_id=2, replica_groups=mesh['grp'=4,'mem'=8] {'mem'}, use_global_device_ids=true, to_apply=%region_4.5.clone | all-reduce | flops 1024 | bytes 8192
  54.4 0.6 dynamic-slice_multiply_fusion
  55.0 0.0 collective-permute-done.2
  55.0 0.0 collective-permute-done.1
  55.0 0.1 pad_maximum_fusion
  55.1 0.6 gather_fusion.1
  55.6 0.0 copy-done
  55.6 6.4 %fusion.2 = f32[1024]{0:T(1024)} fusion(bf16[1024,4096]{1,0:T(8,128)(2,1)} %param.6, bf16[64,4096]{1,0:T(8,128)(2,1)S(1)} %bitcast.32, s32[16]{0:T(128)S(1)} %copy-done), kind=kOutput, calls=%fused_computation.10 | convolution fusion | flops 142704640 | bytes 8917056 | tf_op jit(solution)/shard_map/dot_general | solution.py:45
  (56 shorter events, 0.9 us)
Async XLA Ops:
  0.6 20.4 %slice-start = ((s8[8388608]{0:T(1024)(128)(4,1)}), s8[4194304]{0:T(1024)(128)(4,1)S(1)}, s32[]{:S(2)}) async-start(s8[8388608]{0:T(1024)(128)(4,1)} %bitcast.28), calls=%async_computation | async-start | bytes 8388608
  0.6 16.3 %copy-start.1 = (s32[1,16]{1,0:T(1,128)S(1)}, s32[1,16]{1,0:T(1,128)}, u32[]{:S(2)}) copy-start(s32[1,16]{1,0:T(1,128)} %param.8) | copy-start | bytes 196
  0.7 20.4 %slice-start.1 = ((s8[8388608]{0:T(1024)(128)(4,1)}), s8[4194304]{0:T(1024)(128)(4,1)S(1)}, s32[]{:S(2)}) async-start(s8[8388608]{0:T(1024)(128)(4,1)} %bitcast.28), calls=%async_computation.1 | async-start | bytes 8388608
  17.1 12.3 %collective-permute-start = (bf16[16,4096]{1,0:T(8,128)(2,1)S(1)}, bf16[16,4096]{1,0:T(8,128)(2,1)S(1)}, u32[]{:S(2)}, u32[]{:S(2)}) collective-permute-start(bf16[16,4096]{1,0:T(8,128)(2,1)S(1)} %convolution_convert_fusion.1), channel_id=1, source_target_pairs={{0,8},{8,16},{16,24},{24,0},{1,9},{9,17},{17,25},{25,1},{2,10},{10... | collective-permute-start | bytes 393224 | tf_op jit(solution)/shard_map/ppermute | solution.py:22
  18.8 36.2 %collective-permute-start.2 = (bf16[16,4096]{1,0:T(8,128)(2,1)S(1)}, bf16[16,4096]{1,0:T(8,128)(2,1)S(1)}, u32[]{:S(2)}, u32[]{:S(2)}) collective-permute-start(bf16[16,4096]{1,0:T(8,128)(2,1)S(1)} %convolution_convert_fusion.1), channel_id=1, source_target_pairs={{8,0},{16,8},{24,16},{0,24},{9,1},{17,9},{25,17},{1,25},{10,2},{18... | collective-permute-start | bytes 393224 | tf_op jit(solution)/shard_map/ppermute | solution.py:24
  21.0 8.6 %copy-start.2 = (u32[32]{0:T(128)S(1)}, u32[32]{0:T(128)}, u32[]{:S(2)}) copy-start(u32[32]{0:T(128)} %constant.73) | copy-start | bytes 388
  21.0 34.6 %copy-start = (s32[16]{0:T(128)S(1)}, s32[16]{0:T(128)}, u32[]{:S(2)}) copy-start(s32[16]{0:T(128)} %param.9) | copy-start | bytes 196
  29.5 25.5 %collective-permute-start.1 = (bf16[16,4096]{1,0:T(8,128)(2,1)S(1)}, bf16[16,4096]{1,0:T(8,128)(2,1)S(1)}, u32[]{:S(2)}, u32[]{:S(2)}) collective-permute-start(bf16[16,4096]{1,0:T(8,128)(2,1)S(1)} %collective-permute-done), channel_id=1, source_target_pairs={{0,8},{8,16},{16,24},{24,0},{1,9},{9,17},{17,25},{25,1},{2,10},{10... | collective-permute-start | bytes 393224 | tf_op jit(solution)/shard_map/ppermute | solution.py:22
